TPU v7x, 256 devices: a whole 4x4x8 slice. The times are simulated.
256 devices in a mesh: dp: 16 (over x, z_lo), hyper: 16 (over y, z_hi, core).
Axes of the slice: x: 4, y: 4, z: 8 (z_hi: 2, z_lo: 4; z = z_hi * 4 + z_lo), core: 2. Of those that a mesh axis runs over, the one named last changes fastest.
Arguments:
- inputs: bfloat16 [512, 64, 128], P(('dp', 'hyper')), may hold values from -64 to 64
- labels: int32 [512, 64], P(('dp', 'hyper')), may hold values from 0 to 255
- client_ids: int32 [512], P(('dp', 'hyper')), may hold values from 0 to 511
- ext_weight: bfloat16 [128, 4096], replicated, may hold values from -0.5 to 0.5
- ext_bias: bfloat16 [4096], replicated, may hold values from -3 to 3
- embeddings: bfloat16 [512, 128], replicated, may hold values from -1.5 to 1.5
- hyper_in: bfloat16 [128, 50], replicated, may hold values from -2.09375 to 2.09375
- hyper_bias: float32 [50], replicated, may hold values from -3 to 3
- hyper_out: bfloat16 [4096, 50, 256], P('hyper'), may hold values from -0.1796875 to 0.1796875
Outputs:
- grad_ext_weight: float32 [128, 4096], replicated
- grad_ext_bias: float32 [4096], replicated
- grad_embeddings: float32 [512, 128], replicated
- grad_hyper_in: float32 [128, 50], replicated
- grad_hyper_bias: float32 [50], replicated
- grad_hyper_out: float32 [4096, 50, 256], P(('hyper', 'dp'))
Inputs may be any that keep to these rules, and one draw needn't show every extreme that they name: `client_ids`: A client may hold several slots or none.
All inputs are finite; a program needn't handle non-finite values.
Results may differ from a plain program's by a relative error of at most 0.014.
The roundings to bfloat16 on the way count: a program that leaves them out, or rounds other values in their place, can miss the bound.
Values may be sent and summed in bfloat16 or wider, within the bound.
No kernel may reach another device: no remote copies, remote signals or barrier semaphores. Data moves between devices by JAX's collectives and lax.ppermute only.
A program may use at most 128 MiB of HBM per device.

v0:
```python
import jax
import jax.numpy as jnp
from jax import lax
from jax.sharding import Mesh
from jax.sharding import PartitionSpec as P

DP = ("dp_0", "dp_1")
DP_HYPER = ("dp_0", "dp_1", "hyper")
HYPER_DP = ("hyper", "dp_0", "dp_1")


def sent_to_all(value, axis):
    copies = jnp.broadcast_to(value, (lax.axis_size(axis), *value.shape))
    return lax.all_to_all(copies, axis, split_axis=0, concat_axis=0, tiled=True)


def laid_out(tiles, dim):
    lengths = list(tiles.shape[1:])
    lengths[dim] *= tiles.shape[0]
    return jnp.moveaxis(tiles, 0, dim).reshape(lengths)


def gather_directly(value, axis, dim):
    tiles = sent_to_all(value, axis)
    return laid_out(tiles, dim)


def own_rows(terms, axes):
    total = terms.astype(jnp.bfloat16)
    for axis in axes:
        total = lax.psum_scatter(total, axis, scatter_dimension=0, tiled=True)
    return total.astype(jnp.float32)


def silu_slope(values):
    logistic = jax.nn.sigmoid(values)
    return logistic * (1.0 + values * (1.0 - logistic))


def class_grads(logits, slot_labels, row_count):
    largest = jnp.max(logits, axis=-1, keepdims=True)
    exponent = jnp.exp(logits - largest)
    probability = exponent / jnp.sum(exponent, axis=-1, keepdims=True)
    classes = jnp.arange(logits.shape[-1], dtype=jnp.int32)
    onehot = (slot_labels[..., None] == classes).astype(jnp.float32)
    return ((probability - onehot) / row_count).astype(jnp.bfloat16)


def local(
    inputs, labels, client_ids, ext_weight, ext_bias, embeddings, hyper_in, hyper_bias, hyper_out
):
    slot_count, row_count, width_in = inputs.shape
    width = ext_weight.shape[1]
    flat_in = inputs.reshape(slot_count * row_count, width_in)
    preact = jnp.dot(flat_in, ext_weight, preferred_element_type=jnp.float32) + ext_bias.astype(
        jnp.float32
    )
    features = jax.nn.silu(preact).astype(jnp.bfloat16).reshape(slot_count, row_count, width)
    row_ids = gather_directly(client_ids, "hyper", 0)
    table_ids = jnp.arange(embeddings.shape[0], dtype=jnp.int32)
    select = (row_ids[:, None] == table_ids[None, :]).astype(jnp.bfloat16)
    picked = jnp.dot(select, embeddings, preferred_element_type=jnp.float32).astype(jnp.bfloat16)
    hyper_preact = jnp.dot(picked, hyper_in, preferred_element_type=jnp.float32) + hyper_bias
    hidden = jax.nn.silu(hyper_preact).astype(jnp.bfloat16)
    head_part = jnp.einsum(
        "kh,dhc->kdc", hidden, hyper_out, preferred_element_type=jnp.float32
    ).astype(jnp.bfloat16)
    feat_cols = lax.all_to_all(features, "hyper", split_axis=2, concat_axis=0, tiled=True)
    logits = lax.psum_scatter(
        jnp.einsum("krd,kdc->krc", feat_cols, head_part, preferred_element_type=jnp.float32),
        "hyper",
        scatter_dimension=0,
        tiled=True,
    )
    dlogits = class_grads(logits, labels, row_count)
    dlog_rows = lax.all_gather(dlogits, "hyper", axis=0, tiled=True)
    dhead_part = jnp.einsum(
        "krd,krc->kdc", feat_cols, dlog_rows, preferred_element_type=jnp.float32
    ).astype(jnp.bfloat16)
    dfeat_cols = jnp.einsum(
        "krc,kdc->krd", dlog_rows, head_part, preferred_element_type=jnp.float32
    ).astype(jnp.bfloat16)
    dfeatures = lax.all_to_all(dfeat_cols, "hyper", split_axis=0, concat_axis=2, tiled=True)
    dpreact = (
        dfeatures.reshape(slot_count * row_count, width).astype(jnp.float32) * silu_slope(preact)
    ).astype(jnp.bfloat16)
    grad_weight = jnp.dot(flat_in.T, dpreact, preferred_element_type=jnp.float32)
    grad_bias = jnp.sum(dpreact.astype(jnp.float32), axis=0)
    grad_out = own_rows(
        jnp.einsum("kh,kdc->dhc", hidden, dhead_part, preferred_element_type=jnp.float32), DP
    )
    dhidden = jnp.einsum("kdc,dhc->kh", dhead_part, hyper_out, preferred_element_type=jnp.float32)
    hyper_dpre = dhidden * silu_slope(hyper_preact)
    grad_in = jnp.dot(picked.astype(jnp.float32).T, hyper_dpre)
    grad_hbias = jnp.sum(hyper_dpre, axis=0)
    back_rows = jnp.dot(hyper_dpre, hyper_in.astype(jnp.float32).T)
    grad_table = jnp.dot(select.astype(jnp.float32).T, back_rows)
    grad_weight, grad_bias, grad_table, grad_in, grad_hbias = lax.psum(
        (grad_weight, grad_bias, grad_table, grad_in, grad_hbias), DP_HYPER
    )
    return (grad_weight, grad_bias, grad_table, grad_in, grad_hbias, grad_out)


def solution(mesh):
    torus = Mesh(mesh.devices.reshape(4, 4, mesh.shape["hyper"]), ("dp_0", "dp_1", "hyper"))
    placed = (
        P(DP_HYPER, None, None),
        P(DP_HYPER, None),
        P(DP_HYPER),
        P(),
        P(),
        P(),
        P(),
        P(),
        P("hyper", None, None),
    )
    return jax.shard_map(
        local,
        mesh=torus,
        in_specs=placed,
        out_specs=(P(), P(), P(), P(), P(), P(HYPER_DP, None, None)),
        check_vma=False,
    )
```

profile of v0, /device:TPU:1, one launch (start us, length us, event | category | flops | bytes accessed | tf_op | source)
XLA Modules:
  0.0 629.8 jit_solution(14461696702569586145)
XLA Ops:
  7.2 0.0 copy-start
  7.2 1.3 broadcast_in_dim.2
  8.5 12.6 %all-to-all-start.1 = ((s32[16,1,2]{2,1,0:T(1,128)}), s32[16,1,2]{2,1,0:T(1,128)S(1)}, u32[]{:S(2)}, u32[]{:S(2)}) async-start(s32[16,1,2]{2,1,0:T(1,128)} %broadcast_in_dim.2), calls=%async_computation.1 | async-start | bytes 16384 | tf_op jit(solution)/shard_map/all_to_all | solution.py:14
  21.1 0.7 convert_element_type.58
  21.8 0.0 copy-done
  21.8 3.1 multiply_convert_fusion.1
  24.9 5.0 copy.35
  30.0 0.0 copy-start.8
  30.0 0.0 copy-start.5
  30.0 0.0 copy-start.7
  30.0 2.2 reshape.50
  32.3 0.0 all-to-all-done.1
  32.3 9.6 %all-to-all-start = ((bf16[16,2,16384]{2,1,0:T(2,128)(2,1)}), bf16[16,2,16384]{2,1,0:T(2,128)(2,1)S(1)}, u32[]{:S(2)}, u32[]{:S(2)}) async-start(bf16[16,2,16384]{2,1,0:T(2,128)(2,1)} %reshape.50), calls=%async_computation | async-start | bytes 2097152 | tf_op jit(solution)/shard_map/all_to_all | solution.py:68
  41.9 0.0 reduce-scatter.4.cloned.1.call-start
  41.9 0.5 broadcast.18
  42.4 0.7 reduce.3
  43.1 0.1 eq.28
  43.2 0.0 copy-done.8
  43.2 0.2 convolution_convert_fusion.1
  43.4 0.1 convolution_add_fusion.1
  43.6 10.5 %fusion.9 = bf16[32,256,256]{2,0,1:T(8,128)(2,1)} fusion(bf16[256,50,256]{2,0,1:T(8,128)(2,1)} %param.17, f32[32,50]{1,0:T(8,128)S(1)} %convolution_add_fusion.1), kind=kOutput, calls=%fused_computation.12 | convolution fusion | flops 211820352 | bytes 10754304 | tf_op jit(solution)/shard_map/kh,dhc->kdc/dot_general | solution.py:65
  54.1 9.6 %all-to-all-done = bf16[16,2,16384]{2,1,0:T(2,128)(2,1)S(1)} async-done(((bf16[16,2,16384]{2,1,0:T(2,128)(2,1)}), bf16[16,2,16384]{2,1,0:T(2,128)(2,1)S(1)}, u32[]{:S(2)}, u32[]{:S(2)}) %all-to-all-start) | async-done | bytes 1048608 | tf_op jit(solution)/shard_map/all_to_all | solution.py:68
  63.7 2.4 reshape.51
  66.1 4.5 copy.36
  70.6 6.0 fusion.7
  76.5 0.0 reduce-scatter.4.cloned.1.call-update
  76.6 0.0 all-gather.2.cloned.1.call-start
  76.6 89.9 %reduce-scatter.4.cloned.1.call-done = f32[2,64,256]{2,1,0:T(8,128)} async-done(((f32[32,64,256]{2,1,0:T(8,128)}), f32[2,64,256]{2,1,0:T(8,128)}) %reduce-scatter.4.cloned.1.call-update) | async-done | bytes 131088 | tf_op jit(solution)/shard_map/reduce_scatter | solution.py:69
  166.5 1.9 fusion.20
  168.4 0.0 all-gather.2.cloned.1.call-update
  168.4 0.2 reduce-scatter.6.cloned.1.call-start
  168.7 55.2 %all-gather.2.cloned.1.call-done = bf16[32,64,256]{2,1,0:T(8,128)(2,1)} async-done(((bf16[2,64,256]{2,1,0:T(8,128)(2,1)}), bf16[32,64,256]{2,1,0:T(8,128)(2,1)}) %all-gather.2.cloned.1.call-update) | async-done | bytes 1048592 | tf_op jit(solution)/shard_map/all_gather | solution.py:76
  223.8 2.5 convolution_convert_fusion
  226.4 0.0 copy-start.1
  226.4 2.0 copy-done.1
  228.3 6.0 convert_bitcast_fusion
  234.4 0.0 reduce-scatter.6.cloned.1.call-update
  234.4 1.2 copy-done.2
  235.6 5.7 fusion.12
  241.3 4.0 all-to-all-start.2
  245.3 0.3 all-reduce.4.cloned.1.call-start
  245.6 11.3 %copy.42 = bf16[256,50,256]{0,1,2:T(8,128)(2,1)} copy(bf16[256,50,256]{2,0,1:T(8,128)(2,1)} %param.17) | data formatting | bytes 13107200 | tf_op args[8]
  256.9 8.0 %copy.41 = bf16[32,256,256]{1,0,2:T(8,128)(2,1)} copy(bf16[32,256,256]{2,1,0:T(8,128)(2,1)} %copy-done.1) | data formatting | bytes 8388608 | tf_op jit(solution)/shard_map/convert_element_type | solution.py:79
  264.9 6.5 %fusion.30 = (f32[50]{0:T(128)S(1)}, bf16[32,50]{1,0:T(8,128)(2,1)S(1)}) fusion(f32[32,50]{1,0:T(8,128)S(1)} %convolution_add_fusion.1, bf16[32,256,256]{1,0,2:T(8,128)(2,1)} %copy.41, bf16[256,50,256]{0,1,2:T(8,128)(2,1)} %copy.42), kind=kOutput, calls=%fused_computation.40 | convolution fusion | flops 209731152 | bytes 10757704 | tf_op jit(solution)/shard_map/kdc,dhc->kh/dot_general | solution.py:92
  271.4 1.0 fusion.21
  272.4 0.0 all-to-all-done.2
  272.4 0.6 copy.40
  273.0 0.0 copy-start.3
  273.1 1.7 copy.46
  274.7 0.0 copy-start.6
  274.7 0.8 convert_reduce_fusion
  275.6 0.0 copy-done.6
  275.6 1.8 convolution_bitcast_fusion
  277.4 0.0 all-reduce.4.cloned.1.call-update
  277.4 0.0 reduce-scatter.8.cloned.1.call-start
  277.5 27.3 %reduce-scatter.6.cloned.1.call-done = bf16[64,50,256]{2,1,0:T(8,128)(2,1)} async-done(((bf16[256,50,256]{2,1,0:T(8,128)(2,1)}), bf16[64,50,256]{2,1,0:T(8,128)(2,1)}) %reduce-scatter.6.cloned.1.call-update) | async-done | bytes 1638416 | tf_op jit(solution)/shard_map/reduce_scatter | solution.py:31
  304.8 0.0 reduce-scatter.8.cloned.1.call-update
  304.8 0.2 fusion.31
  305.0 76.7 %all-reduce = (f32[4096]{0:T(1024)}, f32[128,50]{0,1:T(8,128)}, f32[50]{0:T(128)}) all-reduce(f32[4096]{0:T(1024)S(1)} %get-tuple-element.29, f32[128,50]{0,1:T(8,128)S(1)} %fusion.31, f32[50]{0:T(128)S(1)} %get-tuple-element.33), channel_id=1, replica_groups=mesh['dp_0'=4,'dp_1'=4,'hyper'=16] {'dp_0','dp_1','hyper'}, use_global_device_ids=true, to_apply=%region_5.6 | all-reduce | flops 10546 | bytes 84368 | tf_op jit(solution)/shard_map/psum | solution.py:98
  381.7 191.7 %all-reduce.4.cloned.1.call-done = (f32[128,4096]{0,1:T(8,128)}, f32[512,128]{1,0:T(8,128)}) async-done(((f32[128,4096]{0,1:T(8,128)}, f32[512,128]{1,0:T(8,128)}), (f32[128,4096]{0,1:T(8,128)}, f32[512,128]{1,0:T(8,128)})) %all-reduce.4.cloned.1.call-update) | async-done | bytes 2359312 | tf_op jit(solution)/shard_map/psum | solution.py:98
  573.3 2.9 copy.44
  576.3 44.3 %reduce-scatter.8.cloned.1.call-done = bf16[16,50,256]{2,1,0:T(8,128)(2,1)} async-done(((bf16[64,50,256]{2,1,0:T(8,128)(2,1)}), bf16[16,50,256]{2,1,0:T(8,128)(2,1)}) %reduce-scatter.8.cloned.1.call-update) | async-done | bytes 409616 | tf_op jit(solution)/shard_map/reduce_scatter | solution.py:31
  620.6 2.0 copy.45
  622.6 0.7 copy.61
  (8 shorter events, 0.0 us)
Async XLA Ops:
  7.2 14.7 %copy-start = (bf16[128,4096]{1,0:T(8,128)(2,1)S(1)}, bf16[128,4096]{1,0:T(8,128)(2,1)}, u32[]{:S(2)}) copy-start(bf16[128,4096]{1,0:T(8,128)(2,1)} %param.12) | copy-start | bytes 3145732
  8.5 23.7 %all-to-all-start.1 = ((s32[16,1,2]{2,1,0:T(1,128)}), s32[16,1,2]{2,1,0:T(1,128)S(1)}, u32[]{:S(2)}, u32[]{:S(2)}) async-start(s32[16,1,2]{2,1,0:T(1,128)} %broadcast_in_dim.2), calls=%async_computation.1 | async-start | bytes 16384 | tf_op jit(solution)/shard_map/all_to_all | solution.py:14
  30.0 13.2 %copy-start.8 = (bf16[512,128]{1,0:T(8,128)(2,1)S(1)}, bf16[512,128]{1,0:T(8,128)(2,1)}, u32[]{:S(2)}) copy-start(bf16[512,128]{1,0:T(8,128)(2,1)} %param.14) | copy-start | bytes 393220
  30.0 13.4 %copy-start.5 = (bf16[128,50]{0,1:T(8,128)(2,1)S(1)}, bf16[128,50]{0,1:T(8,128)(2,1)}, u32[]{:S(2)}) copy-start(bf16[128,50]{0,1:T(8,128)(2,1)} %param.15) | copy-start | bytes 38404
  30.0 13.4 %copy-start.7 = (f32[50]{0:T(128)S(1)}, f32[50]{0:T(128)}, u32[]{:S(2)}) copy-start(f32[50]{0:T(128)} %param.16) | copy-start | bytes 604
  32.3 31.4 %all-to-all-start = ((bf16[16,2,16384]{2,1,0:T(2,128)(2,1)}), bf16[16,2,16384]{2,1,0:T(2,128)(2,1)S(1)}, u32[]{:S(2)}, u32[]{:S(2)}) async-start(bf16[16,2,16384]{2,1,0:T(2,128)(2,1)} %reshape.50), calls=%async_computation | async-start | bytes 2097152 | tf_op jit(solution)/shard_map/all_to_all | solution.py:68
  41.9 124.6 %reduce-scatter.4.cloned.1.call-start = ((), (), s32[]{:S(2)}) async-start(), calls=%async_computation.6 | async-start | bytes 2228224 | tf_op jit(solution)/shard_map/reduce_scatter | solution.py:69
  76.5 90.0 %copy-start.9 = (s32[2,64]{1,0:T(2,128)S(1)}, s32[2,64]{1,0:T(2,128)}, u32[]{:S(2)}) copy-start(s32[2,64]{1,0:T(2,128)} %param.10) | copy-start | bytes 1540
  76.6 147.3 %all-gather.2.cloned.1.call-start = ((), (), s32[]{:S(2)}) async-start(), calls=%async_computation.7 | async-start | bytes 1114112 | tf_op jit(solution)/shard_map/all_gather | solution.py:76
  168.4 136.4 %reduce-scatter.6.cloned.1.call-start = ((), (), s32[]{:S(2)}) async-start(), calls=%async_computation.8 | async-start | bytes 9175040 | tf_op jit(solution)/shard_map/reduce_scatter | solution.py:31
  226.4 2.0 copy-start.1
  234.4 1.2 copy-start.2
  241.3 31.1 %all-to-all-start.2 = ((bf16[32,64,256]{2,1,0:T(8,128)(2,1)}), bf16[32,64,256]{2,1,0:T(8,128)(2,1)S(1)}, u32[]{:S(2)}, u32[]{:S(2)}) async-start(bf16[32,64,256]{2,1,0:T(8,128)(2,1)} %fusion.12), calls=%async_computation.3 | async-start | bytes 2097152 | tf_op jit(solution)/shard_map/all_to_all | solution.py:83
  245.3 328.0 %all-reduce.4.cloned.1.call-start = ((), (), s32[]{:S(2)}) async-start(), calls=%async_computation.10 | async-start | bytes 4718592 | tf_op jit(solution)/shard_map/psum | solution.py:98
  273.0 1.7 copy-start.3
  274.7 0.8 copy-start.6
  277.4 343.2 %reduce-scatter.8.cloned.1.call-start = ((), (), s32[]{:S(2)}) async-start(), calls=%async_computation.9 | async-start | bytes 2293760 | tf_op jit(solution)/shard_map/reduce_scatter | solution.py:31
  573.3 49.3 %copy-start.4 = (f32[512,128]{1,0:T(8,128)S(1)}, f32[512,128]{1,0:T(8,128)}, u32[]{:S(2)}) copy-start(f32[512,128]{1,0:T(8,128)} %get-tuple-element.39) | copy-start | bytes 786436
Sparse Core Ops, SparseCore 0:
  76.7 89.7 reduce-scatter.3
  169.8 54.0 all-gather.1
  234.5 70.2 reduce-scatter.5
  310.7 262.5 all-reduce.3
  575.7 44.7 reduce-scatter.7
where the time goes:
time: 631 us; the launch traced here: 630 us
  waiting for transfers between devices  418 us (66%)
  blocking collectives  76.7 us (12%)
  local copies, waits for them, and re-layouts  46.5 us (7%)
  matrix products  43.7 us (7%)
  starting transfers between devices  26.8 us (4%)
  between operations  13.9 us (2%)
    psum x1, waiting for transfers between devices, local(): lax.psum((grad_weight, grad_bias, grad_table, grad_in, grad_hbias), DP_HY...  192 us
    reduce_scatter x1, waiting for transfers between devices, local(): lax.psum_scatter(jnp.einsum('krd,kdc->krc', feat_cols, head_part, preferr...  89.9 us
    psum x1, blocking collectives, local(): lax.psum((grad_weight, grad_bias, grad_table, grad_in, grad_hbias), DP_HY...  76.7 us
    reduce_scatter x2, waiting for transfers between devices, own_rows(): total = lax.psum_scatter(total, axis, scatter_dimension=0, tiled=True)  71.6 us
    all_gather x1, waiting for transfers between devices, local(): dlog_rows = lax.all_gather(dlogits, 'hyper', axis=0, tiled=True)  55.2 us
    unnamed x27, local copies, waits for them, and re-layouts  26.5 us
  transfers between devices with their start and end apart: 8, of which 6 were waited for; matrix products, arithmetic and copies ran while one was open for 10% of the time, Pallas kernels for 0%

commit v1 on v0

--- a/solution.py
+++ b/solution.py
@@ -96,7 +96,8 @@
     back_rows = jnp.dot(hyper_dpre, hyper_in.astype(jnp.float32).T)
     grad_table = jnp.dot(select.astype(jnp.float32).T, back_rows)
     grad_weight, grad_bias, grad_table, grad_in, grad_hbias = lax.psum(
-        (grad_weight, grad_bias, grad_table, grad_in, grad_hbias), DP_HYPER
+        lax.psum((grad_weight, grad_bias, grad_table, grad_in, grad_hbias), ("dp_1", "hyper")),
+        "dp_0",
     )
     return (grad_weight, grad_bias, grad_table, grad_in, grad_hbias, grad_out)
 

time: 631 us -> 875 us (1.39)
  the two profiles are of different devices: /device:TPU:1 before, /device:TPU:32 now
where the time goes in v1:
time: 875 us; the launch traced here: 873 us
  waiting for transfers between devices  416 us (48%)
  blocking collectives  329 us (38%)
  matrix products  46.7 us (5%)
  local copies, waits for them, and re-layouts  39.1 us (4%)
  starting transfers between devices  24.8 us (3%)
  between operations  14.3 us (2%)
    psum x1, blocking collectives, local(): lax.psum((grad_weight, grad_bias, grad_table, grad_in, grad_hbias), ('dp_...  311 us
    psum x1, waiting for transfers between devices, local(): lax.psum((grad_weight, grad_bias, grad_table, grad_in, grad_hbias), ('dp_...  181 us
    reduce_scatter x1, waiting for transfers between devices, local(): lax.psum_scatter(jnp.einsum('krd,kdc->krc', feat_cols, head_part, preferr...  81.4 us
    reduce_scatter x2, waiting for transfers between devices, own_rows(): total = lax.psum_scatter(total, axis, scatter_dimension=0, tiled=True)  78.6 us
    all_gather x1, waiting for transfers between devices, local(): dlog_rows = lax.all_gather(dlogits, 'hyper', axis=0, tiled=True)  53.8 us
    unnamed x27, local copies, waits for them, and re-layouts  22.4 us
    all_to_all x1, waiting for transfers between devices, local(): lax.all_to_all(features, 'hyper', split_axis=2, concat_axis=0, tiled=True)  19.6 us
  transfers between devices with their start and end apart: 9, of which 6 were waited for; matrix products, arithmetic and copies ran while one was open for 7% of the time, Pallas kernels for 0%

profile of v1, /device:TPU:32, one launch (start us, length us, event | category | flops | bytes accessed | tf_op | source)
XLA Modules:
  0.0 873.5 jit_solution(16151420607507288877)
XLA Ops:
  7.2 0.0 copy-start
  7.2 1.3 broadcast_in_dim.2
  8.5 10.3 %all-to-all-start.1 = ((s32[16,1,2]{2,1,0:T(1,128)}), s32[16,1,2]{2,1,0:T(1,128)S(1)}, u32[]{:S(2)}, u32[]{:S(2)}) async-start(s32[16,1,2]{2,1,0:T(1,128)} %broadcast_in_dim.2), calls=%async_computation.1 | async-start | bytes 16384 | tf_op jit(solution)/shard_map/all_to_all | solution.py:14
  18.8 0.7 convert_element_type.58
  19.5 3.1 multiply_convert_fusion.1
  22.6 5.0 copy.35
  27.7 0.0 copy-start.8
  27.7 0.0 copy-start.5
  27.7 0.0 copy-start.7
  27.7 2.2 reshape.50
  30.0 0.0 all-to-all-done.1
  30.0 9.6 %all-to-all-start = ((bf16[16,2,16384]{2,1,0:T(2,128)(2,1)}), bf16[16,2,16384]{2,1,0:T(2,128)(2,1)S(1)}, u32[]{:S(2)}, u32[]{:S(2)}) async-start(bf16[16,2,16384]{2,1,0:T(2,128)(2,1)} %reshape.50), calls=%async_computation | async-start | bytes 2097152 | tf_op jit(solution)/shard_map/all_to_all | solution.py:68
  39.6 0.0 reduce-scatter.4.cloned.1.call-start
  39.6 0.5 broadcast.18
  40.2 0.7 reduce.3
  40.8 0.1 eq.28
  40.9 0.0 copy-done.8
  40.9 0.2 convolution_convert_fusion.1
  41.1 0.1 convolution_add_fusion.1
  41.3 10.4 %fusion.9 = bf16[32,256,256]{2,0,1:T(8,128)(2,1)} fusion(bf16[256,50,256]{2,0,1:T(8,128)(2,1)} %param.17, f32[32,50]{1,0:T(8,128)S(1)} %convolution_add_fusion.1), kind=kOutput, calls=%fused_computation.12 | convolution fusion | flops 211820352 | bytes 10754304 | tf_op jit(solution)/shard_map/kh,dhc->kdc/dot_general | solution.py:65
  51.6 19.6 %all-to-all-done = bf16[16,2,16384]{2,1,0:T(2,128)(2,1)S(1)} async-done(((bf16[16,2,16384]{2,1,0:T(2,128)(2,1)}), bf16[16,2,16384]{2,1,0:T(2,128)(2,1)S(1)}, u32[]{:S(2)}, u32[]{:S(2)}) %all-to-all-start) | async-done | bytes 1048608 | tf_op jit(solution)/shard_map/all_to_all | solution.py:68
  71.2 1.3 reshape.51
  72.5 1.2 copy.36
  73.8 5.9 fusion.7
  79.7 0.0 reduce-scatter.4.cloned.1.call-update
  79.7 0.2 all-gather.2.cloned.1.call-start
  80.0 81.4 %reduce-scatter.4.cloned.1.call-done = f32[2,64,256]{2,1,0:T(8,128)} async-done(((f32[32,64,256]{2,1,0:T(8,128)}), f32[2,64,256]{2,1,0:T(8,128)}) %reduce-scatter.4.cloned.1.call-update) | async-done | bytes 131088 | tf_op jit(solution)/shard_map/reduce_scatter | solution.py:69
  161.4 0.0 copy-done.9
  161.4 1.9 fusion.20
  163.3 0.0 all-gather.2.cloned.1.call-update
  163.3 53.8 %all-gather.2.cloned.1.call-done = bf16[32,64,256]{2,1,0:T(8,128)(2,1)} async-done(((bf16[2,64,256]{2,1,0:T(8,128)(2,1)}), bf16[32,64,256]{2,1,0:T(8,128)(2,1)}) %all-gather.2.cloned.1.call-update) | async-done | bytes 1048592 | tf_op jit(solution)/shard_map/all_gather | solution.py:76
  217.1 6.0 fusion.12
  223.1 4.3 all-to-all-start.2
  227.4 0.0 copy-start.2
  227.4 0.0 all-reduce.7.cloned.1.call-start
  227.4 11.4 %copy.42 = bf16[256,50,256]{0,1,2:T(8,128)(2,1)} copy(bf16[256,50,256]{2,0,1:T(8,128)(2,1)} %param.17) | data formatting | bytes 13107200 | tf_op args[8]
  238.8 3.4 convolution_convert_fusion
  242.2 7.9 copy.41
  250.1 6.4 fusion.30
  256.5 1.0 fusion.21
  257.6 1.4 all-to-all-done.2
  258.9 0.6 copy.40
  259.6 0.0 copy-start.3
  259.6 1.7 copy.46
  261.2 0.0 copy-start.6
  261.3 0.8 convert_reduce_fusion
  262.1 0.0 copy-done.6
  262.1 1.8 convolution_bitcast_fusion
  263.9 0.0 all-reduce.7.cloned.1.call-update
  263.9 0.3 reduce-scatter.6.cloned.1.call-start
  264.2 8.2 convert_bitcast_fusion
  272.4 0.0 reduce-scatter.6.cloned.1.call-update
  272.4 0.0 all-reduce.9.cloned.1.call-start
  272.5 181.0 %all-reduce.7.cloned.1.call-done = (f32[128,4096]{0,1:T(8,128)}, f32[512,128]{1,0:T(8,128)}) async-done(((f32[128,4096]{0,1:T(8,128)}, f32[512,128]{1,0:T(8,128)}), (f32[128,4096]{0,1:T(8,128)}, f32[512,128]{1,0:T(8,128)})) %all-reduce.7.cloned.1.call-update) | async-done | bytes 2359312 | tf_op jit(solution)/shard_map/psum | solution.py:99
  453.5 0.0 all-reduce.9.cloned.1.call-update
  453.5 0.0 reduce-scatter.8.cloned.1.call-start
  453.6 78.6 %reduce-scatter.6.cloned.1.call-done = bf16[64,50,256]{2,1,0:T(8,128)(2,1)} async-done(((bf16[256,50,256]{2,1,0:T(8,128)(2,1)}), bf16[64,50,256]{2,1,0:T(8,128)(2,1)}) %reduce-scatter.6.cloned.1.call-update) | async-done | bytes 1638416 | tf_op jit(solution)/shard_map/reduce_scatter | solution.py:31
  532.1 0.0 reduce-scatter.8.cloned.1.call-update
  532.1 0.2 fusion.31
  532.3 311.4 %all-reduce = (f32[4096]{0:T(1024)S(1)}, f32[128,50]{0,1:T(8,128)S(1)}, f32[50]{0:T(128)S(1)}) all-reduce(f32[4096]{0:T(1024)S(1)} %get-tuple-element.34, f32[128,50]{0,1:T(8,128)S(1)} %fusion.31, f32[50]{0:T(128)S(1)} %get-tuple-element.38), channel_id=1, replica_groups=mesh['dp_0'=4,'dp_1'=4,'hyper'=16] {'dp_1','hyper'}, use_global_device_ids=true, to_apply=%region_6.7 | all-reduce | flops 10546 | bytes 84368 | tf_op jit(solution)/shard_map/psum | solution.py:99
  843.7 17.1 %all-reduce.2 = (f32[4096]{0:T(1024)}, f32[128,50]{0,1:T(8,128)}, f32[50]{0:T(128)}) all-reduce(f32[4096]{0:T(1024)S(1)} %get-tuple-element.24, f32[128,50]{0,1:T(8,128)S(1)} %get-tuple-element.25, f32[50]{0:T(128)S(1)} %get-tuple-element.26), channel_id=1, replica_groups=mesh['dp_0'=4,'dp_1'=4,'hyper'=16] {'dp_0'}, use_global_device_ids=true, to_apply=%region_7.8 | all-reduce | flops 10546 | bytes 84368 | tf_op jit(solution)/shard_map/psum | solution.py:98
  860.9 3.0 copy.44
  863.9 2.0 copy.45
  865.9 0.7 copy.63
  (12 shorter events, 0.0 us)
Async XLA Ops:
  7.2 12.4 %copy-start = (bf16[128,4096]{1,0:T(8,128)(2,1)S(1)}, bf16[128,4096]{1,0:T(8,128)(2,1)}, u32[]{:S(2)}) copy-start(bf16[128,4096]{1,0:T(8,128)(2,1)} %param.12) | copy-start | bytes 3145732
  8.5 21.4 %all-to-all-start.1 = ((s32[16,1,2]{2,1,0:T(1,128)}), s32[16,1,2]{2,1,0:T(1,128)S(1)}, u32[]{:S(2)}, u32[]{:S(2)}) async-start(s32[16,1,2]{2,1,0:T(1,128)} %broadcast_in_dim.2), calls=%async_computation.1 | async-start | bytes 16384 | tf_op jit(solution)/shard_map/all_to_all | solution.py:14
  27.7 13.2 %copy-start.8 = (bf16[512,128]{1,0:T(8,128)(2,1)S(1)}, bf16[512,128]{1,0:T(8,128)(2,1)}, u32[]{:S(2)}) copy-start(bf16[512,128]{1,0:T(8,128)(2,1)} %param.14) | copy-start | bytes 393220
  27.7 13.4 %copy-start.5 = (bf16[128,50]{0,1:T(8,128)(2,1)S(1)}, bf16[128,50]{0,1:T(8,128)(2,1)}, u32[]{:S(2)}) copy-start(bf16[128,50]{0,1:T(8,128)(2,1)} %param.15) | copy-start | bytes 38404
  27.7 13.4 %copy-start.7 = (f32[50]{0:T(128)S(1)}, f32[50]{0:T(128)}, u32[]{:S(2)}) copy-start(f32[50]{0:T(128)} %param.16) | copy-start | bytes 604
  30.0 41.2 %all-to-all-start = ((bf16[16,2,16384]{2,1,0:T(2,128)(2,1)}), bf16[16,2,16384]{2,1,0:T(2,128)(2,1)S(1)}, u32[]{:S(2)}, u32[]{:S(2)}) async-start(bf16[16,2,16384]{2,1,0:T(2,128)(2,1)} %reshape.50), calls=%async_computation | async-start | bytes 2097152 | tf_op jit(solution)/shard_map/all_to_all | solution.py:68
  39.6 121.8 %reduce-scatter.4.cloned.1.call-start = ((), (), s32[]{:S(2)}) async-start(), calls=%async_computation.6 | async-start | bytes 2228224 | tf_op jit(solution)/shard_map/reduce_scatter | solution.py:69
  79.7 81.7 %copy-start.9 = (s32[2,64]{1,0:T(2,128)S(1)}, s32[2,64]{1,0:T(2,128)}, u32[]{:S(2)}) copy-start(s32[2,64]{1,0:T(2,128)} %param.10) | copy-start | bytes 1540
  79.7 137.4 %all-gather.2.cloned.1.call-start = ((), (), s32[]{:S(2)}) async-start(), calls=%async_computation.7 | async-start | bytes 1114112 | tf_op jit(solution)/shard_map/all_gather | solution.py:76
  223.1 35.8 %all-to-all-start.2 = ((bf16[32,64,256]{2,1,0:T(8,128)(2,1)}), bf16[32,64,256]{2,1,0:T(8,128)(2,1)S(1)}, u32[]{:S(2)}, u32[]{:S(2)}) async-start(bf16[32,64,256]{2,1,0:T(8,128)(2,1)} %fusion.12), calls=%async_computation.3 | async-start | bytes 2097152 | tf_op jit(solution)/shard_map/all_to_all | solution.py:83
  227.4 11.4 %copy-start.2 = (bf16[32,64,256]{2,1,0:T(8,128)(2,1)S(1)}, bf16[32,64,256]{2,1,0:T(8,128)(2,1)}, u32[]{:S(2)}) copy-start(bf16[32,64,256]{2,1,0:T(8,128)(2,1)} %all-gather.2.cloned.1.call-done) | copy-start | bytes 3145732
  227.4 226.1 %all-reduce.7.cloned.1.call-start = ((), (), s32[]{:S(2)}) async-start(), calls=%async_computation.10 | async-start | bytes 4718592 | tf_op jit(solution)/shard_map/psum | solution.py:99
  259.6 1.7 copy-start.3
  261.2 0.8 copy-start.6
  263.9 268.2 %reduce-scatter.6.cloned.1.call-start = ((), (), s32[]{:S(2)}) async-start(), calls=%async_computation.8 | async-start | bytes 9175040 | tf_op jit(solution)/shard_map/reduce_scatter | solution.py:31
  272.4 588.5 %all-reduce.9.cloned.1.call-start = ((), (), s32[]{:S(2)}) async-start(), calls=%async_computation.11 | async-start | bytes 4718592 | tf_op jit(solution)/shard_map/psum | solution.py:98
  453.5 410.4 %reduce-scatter.8.cloned.1.call-start = ((), (), s32[]{:S(2)}) async-start(), calls=%async_computation.9 | async-start | bytes 2293760 | tf_op jit(solution)/shard_map/reduce_scatter | solution.py:31
  860.9 5.7 copy-start.1
  860.9 5.0 copy-start.4
Sparse Core Ops, SparseCore 0:
  79.9 81.5 reduce-scatter.3
  164.7 52.3 all-gather.1
  264.0 189.3 all-reduce.6
  455.9 76.1 reduce-scatter.5
  534.4 67.7 all-reduce.8
  604.6 44.2 reduce-scatter.7
